TPU v7x, 32 devices: a whole 2x2x4 slice. The times are simulated.
32 devices in a mesh: floor: 4 (over y, x), zone: 8 (over z, core).
Axes of the slice: x: 2, y: 2, z: 4, core: 2. Of those that a mesh axis runs over, the one named last changes fastest.
Arguments:
- factor: float32 [512, 96, 384], P(('floor', 'zone')), may hold values from -0.625 to 0.625
- plant_map: float32 [512, 96, 384], P(('floor', 'zone')), may hold values from -0.4082483 to 0.4082483
- offset: float32 [512, 384], P(('floor', 'zone')), may hold values from -10 to 10
- start_plan: float32 [512, 384], P(('floor', 'zone')), may hold values from -10 to 10
- demand: float32 [4, 48], replicated, may hold values from -768 to 768
- start_price: float32 [4, 48], replicated, may hold values from -6 to 6
- start_multiplier: float32 [512, 48], P(('floor', 'zone')), may hold values from -6 to 6
- neighbors: int32 [512, 4], P(('floor', 'zone')), may hold values from 0 to 127
- loop_of_zone: int32 [512], P(('floor', 'zone')), may hold values from 0 to 3
Outputs:
- control: float32 [512, 384], P(('floor', 'zone'))
- price: float32 [4, 48], replicated
- multiplier: float32 [512, 48], P(('floor', 'zone'))
Inputs may be any that keep to these rules, and one draw needn't show every extreme that they name: `neighbors`: indices count zones within the zone's own floor of 128 consecutive zones.
All inputs are finite; a program needn't handle non-finite values.
Results may differ from a plain program's by a relative error of at most 0.0001.
Values sent between devices are 32-bit elements; how exact they have to be, the bound alone decides.
A program may use at most 64 MiB of HBM per device.

v0:
```python
import jax
import jax.numpy as jnp
from jax import lax
from jax.sharding import PartitionSpec as P

HORIZON = 48
NEIGHBORS = 4
LOOPS = 4
ITERS = 2


def select_rows(neighbors, count):
    columns = jnp.arange(count, dtype=jnp.int32)
    picks = (neighbors[:, :, None] == columns[None, None, :]).astype(jnp.float32)
    return jnp.sum(picks, axis=1) / NEIGHBORS


def local(
    factor,
    plant_map,
    offset,
    start_plan,
    demand,
    start_price,
    start_multiplier,
    neighbors,
    loop_of_zone,
):
    control = start_plan
    price = start_price
    multiplier = start_multiplier
    zones_here = control.shape[0]
    zones_all = zones_here * lax.axis_size("floor") * lax.axis_size("zone")
    onehot = (loop_of_zone[:, None] == jnp.arange(LOOPS, dtype=jnp.int32)[None, :]).astype(
        jnp.float32
    )
    for step in range(ITERS):
        outputs = jnp.einsum("zkv,zv->zk", plant_map, control, precision=lax.Precision.HIGHEST)
        shares = outputs[:, :HORIZON]
        bound = outputs[:, HORIZON:]
        partial_load = jnp.dot(onehot.T, shares, precision=lax.Precision.HIGHEST)
        floor_load = lax.psum(partial_load, "zone")
        total = lax.psum(floor_load, "floor")
        excess = (total - demand) * (LOOPS / zones_all)
        shift = jnp.dot(onehot, excess + price, precision=lax.Precision.HIGHEST)
        price = price + excess
        target_share = shares - shift
        floor_bound = lax.all_gather(bound, "zone", axis=0, tiled=True)
        weights = select_rows(neighbors, floor_bound.shape[0])
        near = jnp.dot(weights, floor_bound, precision=lax.Precision.HIGHEST)
        target_bound = (bound + near) / 2.0 - multiplier
        multiplier = multiplier + (bound - near) / 2.0
        target = jnp.concatenate([target_share, target_bound], axis=1)
        control = (
            0.8 * jnp.einsum("zkv,zk->zv", factor, target, precision=lax.Precision.HIGHEST) - offset
        )
    return (control, price, multiplier)


def solution(mesh):
    placed = (
        P(("floor", "zone"), None, None),
        P(("floor", "zone"), None, None),
        P(("floor", "zone"), None),
        P(("floor", "zone"), None),
        P(),
        P(),
        P(("floor", "zone"), None),
        P(("floor", "zone"), None),
        P(("floor", "zone")),
    )
    return jax.shard_map(
        local,
        mesh=mesh,
        in_specs=placed,
        out_specs=(P(("floor", "zone"), None), P(), P(("floor", "zone"), None)),
        check_vma=False,
    )
```

profile of v0, /device:TPU:0, one launch (start us, length us, event | category | flops | bytes accessed | tf_op | source)
XLA Modules:
  0.0 91.8 jit_solution(17976281189199001725)
XLA Ops:
  0.6 0.0 copy-start
  0.6 0.0 copy-start.3
  0.7 0.0 copy-start.4
  0.7 0.0 copy-start.8
  0.7 0.0 copy-start.5
  0.7 0.0 copy-start.6
  0.7 0.0 copy-start.2
  0.7 4.4 %fusion.5 = f32[16,1,96]{2,1,0:T(1,128)S(1)} fusion(f32[16,96,384]{2,1,0:T(8,128)} %param.10, f32[16,384,1]{1,0,2:T(8,128)} %bitcast.43), kind=kOutput, calls=%fused_computation.11 | convolution fusion | flops 7077888 | bytes 2390016 | tf_op jit(solution)/shard_map/zkv,zv->zk/dot_general | solution.py:38
  5.1 0.1 slice.17
  5.2 15.7 %all_gather.6 = f32[128,48]{1,0:T(8,128)S(1)} all-gather(f32[16,48]{1,0:T(8,128)S(1)} %slice.17), channel_id=1, replica_groups=mesh['floor'=4,'zone'=8] {'zone'}, dimensions={0}, use_global_device_ids=true | all-gather | bytes 27648 | tf_op jit(solution)/shard_map/all_gather | solution.py:48
  20.9 0.0 copy-done.4
  20.9 0.1 convert_reduce_fusion
  21.0 0.0 copy-done.3
  21.0 0.2 multiply_subtract_fusion.1
  21.1 0.0 copy-done.8
  21.1 0.3 fusion.8
  21.4 16.9 %psum.28 = f32[4,48]{1,0:T(4,128)S(1)} all-reduce(f32[4,48]{1,0:T(4,128)S(1)} %fusion.8), channel_id=1, replica_groups=mesh['floor'=4,'zone'=8] {'zone'}, use_global_device_ids=true, to_apply=%region_0.0 | all-reduce | flops 192 | bytes 1536 | tf_op jit(solution)/shard_map/psum | solution.py:42
  38.3 9.9 %psum.29 = f32[4,48]{1,0:T(4,128)S(1)} all-reduce(f32[4,48]{1,0:T(4,128)S(1)} %psum.28), channel_id=1, replica_groups=mesh['floor'=4,'zone'=8] {'floor'}, use_global_device_ids=true, to_apply=%region_1.0 | all-reduce | flops 192 | bytes 1536 | tf_op jit(solution)/shard_map/psum | solution.py:43
  48.2 0.0 copy-done.5
  48.2 0.0 copy-done.6
  48.2 0.0 copy-start.1
  48.2 0.2 convolution_subtract_fusion.1
  48.4 0.1 pad_maximum_fusion
  48.5 0.0 copy-done
  48.5 1.4 %fusion.24 = f32[16,1,384]{2,1,0:T(1,128)S(1)} fusion(f32[16,96,1]{1,2,0:T(1,128)S(1)} %bitcast.41, f32[16,96,384]{2,1,0:T(8,128)S(1)} %copy-done), kind=kOutput, calls=%fused_computation.39 | convolution fusion | flops 7077888 | bytes 2390016 | tf_op jit(solution)/shard_map/zkv,zk->zv/dot_general | solution.py:55
  49.9 0.0 copy-done.2
  49.9 0.0 copy-done.1
  49.9 2.6 %fusion.3 = f32[16,1,96]{2,1,0:T(1,128)S(1)} fusion(f32[16,96,384]{2,1,0:T(8,128)S(1)} %copy-done.1, f32[16,384,1]{1,0,2:T(8,128)S(1)} %fusion.2), kind=kOutput, calls=%fused_computation.9 | convolution fusion | flops 7077888 | bytes 2390016 | tf_op jit(solution)/shard_map/zkv,zv->zk/dot_general | solution.py:38
  52.5 0.1 slice.19
  52.6 14.0 %all_gather.7 = f32[128,48]{1,0:T(8,128)S(1)} all-gather(f32[16,48]{1,0:T(8,128)S(1)} %slice.19), channel_id=1, replica_groups=mesh['floor'=4,'zone'=8] {'zone'}, dimensions={0}, use_global_device_ids=true | all-gather | bytes 27648 | tf_op jit(solution)/shard_map/all_gather | solution.py:48
  66.6 0.8 multiply_add_fusion
  67.4 0.3 fusion.7
  67.6 13.9 %psum.30 = f32[4,48]{1,0:T(4,128)S(1)} all-reduce(f32[4,48]{1,0:T(4,128)S(1)} %fusion.7), channel_id=1, replica_groups=mesh['floor'=4,'zone'=8] {'zone'}, use_global_device_ids=true, to_apply=%region_3.0 | all-reduce | flops 192 | bytes 1536 | tf_op jit(solution)/shard_map/psum | solution.py:42
  81.5 7.9 %psum.31 = f32[4,48]{1,0:T(4,128)S(1)} all-reduce(f32[4,48]{1,0:T(4,128)S(1)} %psum.30), channel_id=1, replica_groups=mesh['floor'=4,'zone'=8] {'floor'}, use_global_device_ids=true, to_apply=%region_4.0 | all-reduce | flops 192 | bytes 1536 | tf_op jit(solution)/shard_map/psum | solution.py:43
  89.5 0.0 copy-start.7
  89.5 0.2 convolution_subtract_fusion
  89.7 0.1 pad_maximum_fusion.1
  89.8 1.4 %fusion.25 = f32[16,1,384]{2,1,0:T(1,128)S(1)} fusion(f32[16,96,1]{1,2,0:T(1,128)S(1)} %bitcast.42, f32[16,96,384]{2,1,0:T(8,128)S(1)} %copy-done), kind=kOutput, calls=%fused_computation.40 | convolution fusion | flops 7077888 | bytes 2390016 | tf_op jit(solution)/shard_map/zkv,zk->zv/dot_general | solution.py:55
  91.2 0.6 fusion
  91.8 0.0 copy-done.7
  (2 shorter events, 0.0 us)
Async XLA Ops:
  0.6 47.8 %copy-start = (f32[16,96,384]{2,1,0:T(8,128)S(1)}, f32[16,96,384]{2,1,0:T(8,128)}, u32[]{:S(2)}) copy-start(f32[16,96,384]{2,1,0:T(8,128)} %param.9) | copy-start | bytes 7077892
  0.6 20.3 %copy-start.3 = (f32[16,48]{1,0:T(8,128)S(1)}, f32[16,48]{1,0:T(8,128)}, u32[]{:S(2)}) copy-start(f32[16,48]{1,0:T(8,128)} %param.15) | copy-start | bytes 9220
  0.7 20.2 %copy-start.4 = (s32[16,4]{0,1:T(4,128)S(1)}, s32[16,4]{0,1:T(4,128)}, u32[]{:S(2)}) copy-start(s32[16,4]{0,1:T(4,128)} %param.16) | copy-start | bytes 772
  0.7 20.5 %copy-start.8 = (s32[16]{0:T(128)S(1)}, s32[16]{0:T(128)}, u32[]{:S(2)}) copy-start(s32[16]{0:T(128)} %param.17) | copy-start | bytes 196
  0.7 47.5 %copy-start.5 = (f32[4,48]{1,0:T(4,128)S(1)}, f32[4,48]{1,0:T(4,128)}, u32[]{:S(2)}) copy-start(f32[4,48]{1,0:T(4,128)} %param.14) | copy-start | bytes 2308
  0.7 47.5 %copy-start.6 = (f32[4,48]{1,0:T(4,128)S(1)}, f32[4,48]{1,0:T(4,128)}, u32[]{:S(2)}) copy-start(f32[4,48]{1,0:T(4,128)} %param.13) | copy-start | bytes 2308
  0.7 49.2 %copy-start.2 = (f32[16,384]{1,0:T(8,128)S(1)}, f32[16,384]{1,0:T(8,128)}, u32[]{:S(2)}) copy-start(f32[16,384]{1,0:T(8,128)} %param.11) | copy-start | bytes 73732
  48.2 1.7 %copy-start.1 = (f32[16,96,384]{2,1,0:T(8,128)S(1)}, f32[16,96,384]{2,1,0:T(8,128)}, u32[]{:S(2)}) copy-start(f32[16,96,384]{2,1,0:T(8,128)} %param.10) | copy-start | bytes 7077892
  89.5 2.3 %copy-start.7 = (f32[4,48]{1,0:T(4,128)}, f32[4,48]{1,0:T(4,128)S(1)}, u32[]{:S(2)}) copy-start(f32[4,48]{1,0:T(4,128)S(1)} %multiply_add_fusion.2) | copy-start | bytes 2308
where the time goes:
time: 92.1 us; the launch traced here: 91.8 us
  blocking collectives  78.3 us (85%)
  matrix products  11.7 us (13%)
    psum x2, blocking collectives, local(): floor_load = lax.psum(partial_load, 'zone')  30.8 us
    all_gather x2, blocking collectives, local(): floor_bound = lax.all_gather(bound, 'zone', axis=0, tiled=True)  29.7 us
    psum x2, blocking collectives, local(): total = lax.psum(floor_load, 'floor')  17.8 us
    dot_general x2, matrix products, local(): jnp.einsum('zkv,zv->zk', plant_map, control, precision=lax.Precision.HIGH...  7 us
    dot_general x2, matrix products, local(): jnp.einsum('zkv,zk->zv', factor, target, precision=lax.Precision.HIGHEST)  2.88 us

commit v1 on v0

v1 whole, which is shorter than its diff:
```python
import functools

import jax
import jax.numpy as jnp
from jax import lax
from jax.experimental import pallas as pl
from jax.experimental.pallas import tpu as pltpu
from jax.sharding import PartitionSpec as P

ITERS = 2
MESH = pl.DeviceIdType.MESH
SUB, LANE = 8, 128
CHUNKS = 4


def pieces(x):
    high = x.astype(jnp.bfloat16)
    rest = x - high.astype(jnp.float32)
    mid = rest.astype(jnp.bfloat16)
    low = rest - mid.astype(jnp.float32)
    zero = jnp.zeros_like(low)
    return jnp.concatenate(
        [high.astype(jnp.float32), mid.astype(jnp.float32), low, zero], axis=0
    ).astype(jnp.bfloat16)


def exact_dot(x, picks):
    parts = jnp.dot(pieces(x), picks, preferred_element_type=jnp.float32)
    return parts[:SUB] + parts[SUB : 2 * SUB] + parts[2 * SUB : 3 * SUB]


def kernel(
    floors,
    cols,
    zones_all,
    factor_ref,
    plant_ref,
    offset_ref,
    plan_ref,
    demand_ref,
    price_ref,
    mult_ref,
    near_ref,
    loop_ref,
    control_out,
    price_out,
    mult_out,
    factor,
    plant,
    control,
    select,
    message,
    heard,
    floor_message,
    floor_heard,
    plant_sem,
    factor_sem,
    send_sem,
    recv_sem,
    floor_send_sem,
    floor_recv_sem,
):
    zones, rows, width = plant.shape
    horizon = rows // 2
    groups = horizon // SUB
    loops = demand_ref.shape[0]
    base = groups * zones
    my_floor, me = lax.axis_index("floor"), lax.axis_index("zone")

    step_zones = zones // CHUNKS
    plant_copies, factor_copies = [], []
    for i in range(CHUNKS):
        part = pl.ds(i * step_zones, step_zones)
        plant_copies.append(pltpu.make_async_copy(plant_ref.at[part], plant.at[part], plant_sem.at[i]))
        factor_copies.append(
            pltpu.make_async_copy(factor_ref.at[part], factor.at[part], factor_sem.at[i])
        )
    for copy in plant_copies + factor_copies:
        copy.start()

    zone_peers = [(my_floor, lax.rem(me + d, cols)) for d in range(1, cols)]
    floor_peers = [(lax.rem(my_floor + d, floors), me) for d in range(1, floors)]
    barrier = pltpu.get_barrier_semaphore()
    for peer in zone_peers + floor_peers:
        pl.semaphore_signal(barrier, inc=1, device_id=peer, device_id_type=MESH)

    lane = lax.broadcasted_iota(jnp.int32, (SUB, LANE), 1)

    def pack(x, start):
        count = x.shape[0]
        row = lax.broadcasted_iota(jnp.int32, (count, LANE), 0)
        col = lax.broadcasted_iota(jnp.int32, (count, LANE), 1) - start
        inside = (col >= 0) & (col < groups * count)
        spread = ((lax.rem(jnp.maximum(col, 0), count) == row) & inside).astype(jnp.float32)
        wide = lax.dot_general(
            x, spread, (((0,), (0,)), ((), ())),
            precision=lax.Precision.HIGHEST, preferred_element_type=jnp.float32,
        )
        out = jnp.zeros((SUB, LANE), jnp.float32)
        for j in range(groups):
            first = start + count * j
            mine = (lane >= first) & (lane < first + count)
            out = jnp.where(mine, wide[SUB * j : SUB * (j + 1)], out)
        return out

    def unpack(tile, count, start):
        row = lax.broadcasted_iota(jnp.int32, (count, LANE), 0)
        col = lax.broadcasted_iota(jnp.int32, (count, LANE), 1) - start
        inside = (col >= 0) & (col < groups * count)
        spread = ((lax.rem(jnp.maximum(col, 0), count) == row) & inside).astype(jnp.float32)
        parts = []
        for j in range(groups):
            first = start + count * j
            mine = (lane >= first) & (lane < first + count)
            parts.append(jnp.where(mine, tile, 0.0))
        tall = jnp.concatenate(parts, axis=0)
        return lax.dot_general(
            spread, tall, (((1,), (1,)), ((), ())),
            precision=lax.Precision.HIGHEST, preferred_element_type=jnp.float32,
        )

    is_load = (lane >= base) & (lane < base + groups * loops)
    demand = pack(demand_ref[...], base)
    price = pack(price_ref[...], base)
    mult = pack(mult_ref[...], 0)

    row = lax.broadcasted_iota(jnp.int32, (LANE, LANE), 0)
    col = lax.broadcasted_iota(jnp.int32, (LANE, LANE), 1)
    wide_lane = lax.broadcasted_iota(jnp.int32, (1, LANE), 1)
    lane_zone = lax.rem(wide_lane, zones)
    same = (row // zones == col // zones) & (row < base) & (col < base)
    count = near_ref.shape[1]
    names = []
    for b in range(count):
        value = jnp.zeros((1, LANE), jnp.int32)
        for z in range(zones):
            value = jnp.where(lane_zone == z, near_ref[z, b], value)
        names.append(jnp.broadcast_to(value, (LANE, LANE)))
    inner = lax.rem(row, zones)
    for d in range(cols):
        owner = lax.rem(me - d + cols, cols)
        target = inner + owner * zones
        hits = jnp.zeros((LANE, LANE), jnp.float32)
        for b in range(count):
            hits += (names[b] == target).astype(jnp.float32)
        select[d * LANE : (d + 1) * LANE, :] = jnp.where(same, hits / count, 0.0).astype(jnp.bfloat16)
    loop_lane = jnp.zeros((1, LANE), jnp.int32)
    for z in range(zones):
        loop_lane = jnp.where(lane_zone == z, loop_ref[z], loop_lane)
    wanted = base + (col // zones) * loops + jnp.broadcast_to(loop_lane, (LANE, LANE))
    loop_pick = ((row == wanted) & (col < base)).astype(jnp.float32).astype(jnp.bfloat16)

    loop_of = [loop_ref[z] for z in range(zones)]
    slots = cols - 1
    floor_slots = floors - 1
    sends = []
    for step in range(ITERS):
        source = plan_ref if step == 0 else control
        shares = jnp.zeros((SUB, LANE), jnp.float32)
        tile = jnp.zeros((SUB, LANE), jnp.float32)
        loads = jnp.zeros((SUB, LANE), jnp.float32)
        for z in range(zones):
            if step == 0 and z % step_zones == 0:
                plant_copies[z // step_zones].wait()
            product = plant[z] * source[z : z + 1, :]
            partial = product[:, :LANE]
            for c in range(1, width // LANE):
                partial += product[:, c * LANE : (c + 1) * LANE]
            sums = jnp.sum(partial, axis=1, keepdims=True)
            for j in range(groups):
                share = jnp.broadcast_to(sums[SUB * j : SUB * (j + 1)], (SUB, LANE))
                first = horizon + SUB * j
                bound = jnp.broadcast_to(sums[first : first + SUB], (SUB, LANE))
                mine = lane == zones * j + z
                shares = jnp.where(mine, share, shares)
                tile = jnp.where(mine, bound, tile)
                loads += jnp.where(lane == base + loops * j + loop_of[z], share, 0.0)
        tile = tile + loads
        message[step] = tile
        if step == 0:
            pl.semaphore_wait(barrier, slots + floor_slots)
        for d in range(1, cols):
            copy = pltpu.make_async_remote_copy(
                src_ref=message.at[step],
                dst_ref=heard.at[step, d - 1],
                send_sem=send_sem.at[step, d - 1],
                recv_sem=recv_sem.at[step, d - 1],
                device_id=zone_peers[d - 1],
                device_id_type=MESH,
            )
            copy.start()
            sends.append(copy)
        for copy in sends[len(sends) - slots :]:
            copy.wait_recv()
        floor_tile = tile
        for d in range(slots):
            floor_tile += heard[step, d]
        floor_message[step] = floor_tile
        floor_sends = []
        for d in range(1, floors):
            copy = pltpu.make_async_remote_copy(
                src_ref=floor_message.at[step],
                dst_ref=floor_heard.at[step, d - 1],
                send_sem=floor_send_sem.at[step, d - 1],
                recv_sem=floor_recv_sem.at[step, d - 1],
                device_id=floor_peers[d - 1],
                device_id_type=MESH,
            )
            copy.start()
            floor_sends.append(copy)
        everyone = jnp.concatenate([tile] + [heard[step, d] for d in range(slots)], axis=1)
        near = exact_dot(everyone, select[...])
        here = jnp.where(lane < base, tile, 0.0)
        target_bound = (here + near) * 0.5 - mult
        mult = mult + (here - near) * 0.5
        for copy in floor_sends:
            copy.wait_recv()
        sends += floor_sends
        total = floor_tile
        for d in range(floor_slots):
            total += floor_heard[step, d]
        excess = jnp.where(is_load, (total - demand) * (loops / zones_all), 0.0)
        target_share = shares - exact_dot(excess + price, loop_pick)
        price = price + excess
        for z in range(zones):
            if step == 0 and z % step_zones == 0:
                factor_copies[z // step_zones].wait()
            total_z = jnp.zeros((SUB, width), jnp.float32)
            for half, target in enumerate((target_share, target_bound)):
                for j in range(groups):
                    at = zones * j + z
                    column = jnp.broadcast_to(target[:, at : at + 1], (SUB, width))
                    first = half * horizon + SUB * j
                    total_z += factor[z, first : first + SUB, :] * column
            result = 0.8 * jnp.sum(total_z, axis=0, keepdims=True) - offset_ref[z : z + 1, :]
            if step == ITERS - 1:
                control_out[z : z + 1, :] = result
            else:
                control[z : z + 1, :] = result
    price_out[...] = unpack(price, loops, base)
    mult_out[...] = unpack(mult, zones, 0)
    for copy in sends:
        copy.wait_send()


def solution(mesh):
    floors, cols = mesh.shape["floor"], mesh.shape["zone"]

    def local(factor, plant, offset, plan, demand, price, mult, near, loop):
        zones = plan.shape[0]
        assert (zones + loop_count(demand)) * demand.shape[1] // SUB <= LANE
        vmem, smem = pl.BlockSpec(memory_space=pltpu.VMEM), pl.BlockSpec(memory_space=pltpu.SMEM)
        anywhere = pl.BlockSpec(memory_space=pl.ANY)
        dma = pltpu.SemaphoreType.DMA
        tile = (SUB, LANE)
        return pl.pallas_call(
            functools.partial(kernel, floors, cols, zones * floors * cols),
            out_shape=tuple(jax.ShapeDtypeStruct(x.shape, x.dtype) for x in (plan, price, mult)),
            in_specs=[anywhere, anywhere, vmem, vmem, vmem, vmem, vmem, smem, smem],
            out_specs=(vmem, vmem, vmem),
            scratch_shapes=[
                pltpu.VMEM(factor.shape, jnp.float32),
                pltpu.VMEM(plant.shape, jnp.float32),
                pltpu.VMEM(plan.shape, jnp.float32),
                pltpu.VMEM((cols * LANE, LANE), jnp.bfloat16),
                pltpu.VMEM((ITERS,) + tile, jnp.float32),
                pltpu.VMEM((ITERS, cols - 1) + tile, jnp.float32),
                pltpu.VMEM((ITERS,) + tile, jnp.float32),
                pltpu.VMEM((ITERS, floors - 1) + tile, jnp.float32),
                dma((CHUNKS,)),
                dma((CHUNKS,)),
                dma((ITERS, cols - 1)),
                dma((ITERS, cols - 1)),
                dma((ITERS, floors - 1)),
                dma((ITERS, floors - 1)),
            ],
            compiler_params=pltpu.CompilerParams(collective_id=0, has_side_effects=True),
        )(factor, plant, offset, plan, demand, price, mult, near, loop)

    def loop_count(demand):
        return demand.shape[0]

    both = ("floor", "zone")
    placed = (
        P(both, None, None), P(both, None, None), P(both, None), P(both, None),
        P(), P(), P(both, None), P(both, None), P(both),
    )
    return jax.shard_map(
        local,
        mesh=mesh,
        in_specs=placed,
        out_specs=(P(both, None), P(), P(both, None)),
        check_vma=False,
    )
```

time: 92.1 us -> 28.3 us (0.31)
  blocking collectives: 78.3 us -> 0 us
  Pallas kernels: 0 us -> 22.1 us
  matrix products: 11.7 us -> 0 us
  local copies, waits for them, and re-layouts: 0.2 us -> 5.23 us
    psum x4 -> x0, blocking collectives: 48.6 us -> none  [the longest x2 30.8 us: local(): floor_load = lax.psum(partial_load, 'zone')]
    all_gather x2 -> x0, blocking collectives: 29.7 us -> none  [local(): floor_bound = lax.all_gather(bound, 'zone', axis=0, tiled=True)]
    pallas_call x0 -> x1, Pallas kernels: none -> 22.1 us  [local(): pl.pallas_call(functools.partial(kernel, floors, cols, zones * floors * c...]
    dot_general x10 -> x0, matrix products: 11.7 us -> none  [the longest x2 7 us: local(): jnp.einsum('zkv,zv->zk', plant_map, control, precision=lax.Precision.HIGH...]
    unnamed x18 -> x4, local copies, waits for them, and re-layouts: 0.05 us -> 5.23 us
where the time goes in v1:
time: 28.3 us; the launch traced here: 28 us
  Pallas kernels  22.1 us (78%)
  local copies, waits for them, and re-layouts  5.23 us (18%)
  between operations  0.64 us (2%)
    pallas_call x1, Pallas kernels, local(): pl.pallas_call(functools.partial(kernel, floors, cols, zones * floors * c...  22.1 us
    unnamed x4, local copies, waits for them, and re-layouts  5.23 us

profile of v1, /device:TPU:0, one launch (start us, length us, event | category | flops | bytes accessed | tf_op | source)
XLA Modules:
  0.0 28.0 jit_solution(8807485389938096966)
XLA Ops:
  0.6 1.4 %copy.12.near_ref = s32[16,4]{1,0:T(8,128)} copy(s32[16,4]{0,1:T(4,128)} %param.16) | data formatting | bytes 512 | tf_op args[7]
  2.0 22.1 %shard_map.112 = (f32[16,384]{1,0:T(8,128)}, f32[4,48]{1,0:T(4,128)}, f32[16,48]{1,0:T(8,128)}) custom-call(f32[16,96,384]{2,1,0:T(8,128)} %factor_ref.1, f32[16,96,384]{2,1,0:T(8,128)} %plant_ref.1, f32[16,384]{1,0:T(8,128)} %offset_ref.1, f32[16,384]{1,0:T(8,128)} %plan_ref.1, f32[4,48]{1,0:T(4,128)} %demand_ref.1, f32[4,48]{1,0:T(4,128)} %price_ref.1, ...), custom_call_target="tpu_custom_call" | custom-call | tf_op jit(solution)/shard_map/pallas_call | solution.py:256
  24.1 1.3 %copy.16 = f32[16,384]{1,0:T(8,128)} copy(f32[16,384]{1,0:T(8,128)} %get-tuple-element.6) | data formatting | bytes 49152
  25.4 1.2 %copy.17 = f32[4,48]{1,0:T(4,128)} copy(f32[4,48]{1,0:T(4,128)} %get-tuple-element.7) | data formatting | bytes 1536
  26.7 1.3 %copy.18 = f32[16,48]{1,0:T(8,128)} copy(f32[16,48]{1,0:T(8,128)} %get-tuple-element.8) | data formatting | bytes 6144

commit v2 on v1

--- a/solution.py
+++ b/solution.py
@@ -129,12 +129,12 @@
     wide_lane = lax.broadcasted_iota(jnp.int32, (1, LANE), 1)
     lane_zone = lax.rem(wide_lane, zones)
     same = (row // zones == col // zones) & (row < base) & (col < base)
-    count = near_ref.shape[1]
+    count = near_ref.shape[0]
     names = []
     for b in range(count):
         value = jnp.zeros((1, LANE), jnp.int32)
         for z in range(zones):
-            value = jnp.where(lane_zone == z, near_ref[z, b], value)
+            value = jnp.where(lane_zone == z, near_ref[b, z], value)
         names.append(jnp.broadcast_to(value, (LANE, LANE)))
     inner = lax.rem(row, zones)
     for d in range(cols):
@@ -243,6 +243,11 @@
         copy.wait_send()
 
 
+def hand_over(*refs):
+    for source, target in zip(refs[:3], refs[3:]):
+        target[...] = source[...]
+
+
 def solution(mesh):
     floors, cols = mesh.shape["floor"], mesh.shape["zone"]
 
@@ -253,7 +258,7 @@
         anywhere = pl.BlockSpec(memory_space=pl.ANY)
         dma = pltpu.SemaphoreType.DMA
         tile = (SUB, LANE)
-        return pl.pallas_call(
+        results = pl.pallas_call(
             functools.partial(kernel, floors, cols, zones * floors * cols),
             out_shape=tuple(jax.ShapeDtypeStruct(x.shape, x.dtype) for x in (plan, price, mult)),
             in_specs=[anywhere, anywhere, vmem, vmem, vmem, vmem, vmem, smem, smem],
@@ -275,7 +280,13 @@
                 dma((ITERS, floors - 1)),
             ],
             compiler_params=pltpu.CompilerParams(collective_id=0, has_side_effects=True),
-        )(factor, plant, offset, plan, demand, price, mult, near, loop)
+        )(factor, plant, offset, plan, demand, price, mult, near.T, loop)
+        return pl.pallas_call(
+            hand_over,
+            out_shape=tuple(jax.ShapeDtypeStruct(x.shape, x.dtype) for x in results),
+            in_specs=[vmem] * 3,
+            out_specs=(vmem,) * 3,
+        )(*results)
 
     def loop_count(demand):
         return demand.shape[0]

time: 28.3 us -> 24.3 us (0.86)
  local copies, waits for them, and re-layouts: 5.23 us -> 0 us
  Pallas kernels: 22.1 us -> 23.4 us
    unnamed x4 -> x0, local copies, waits for them, and re-layouts: 5.23 us -> none
    pallas_call x0 -> x1, Pallas kernels: none -> 1.36 us  [local(): pl.pallas_call(hand_over, out_shape=tuple((jax.ShapeDtypeStruct(x.shape,...]
where the time goes in v2:
time: 24.3 us; the launch traced here: 24 us
  Pallas kernels  23.4 us (96%)
  between operations  0.64 us (3%)
    pallas_call x1, Pallas kernels, local(): pl.pallas_call(functools.partial(kernel, floors, cols, zones * floors * c...  22 us
    pallas_call x1, Pallas kernels, local(): pl.pallas_call(hand_over, out_shape=tuple((jax.ShapeDtypeStruct(x.shape,...  1.36 us

profile of v2, /device:TPU:0, one launch (start us, length us, event | category | flops | bytes accessed | tf_op | source)
XLA Modules:
  0.0 24.0 jit_solution(3855050842555396847)
XLA Ops:
  0.6 22.0 %shard_map.112 = (f32[16,384]{1,0:T(8,128)}, f32[4,48]{1,0:T(4,128)}, f32[16,48]{1,0:T(8,128)}) custom-call(f32[16,96,384]{2,1,0:T(8,128)} %factor_ref.1, f32[16,96,384]{2,1,0:T(8,128)} %plant_ref.1, f32[16,384]{1,0:T(8,128)} %offset_ref.1, f32[16,384]{1,0:T(8,128)} %plan_ref.1, f32[4,48]{1,0:T(4,128)} %demand_ref.1, f32[4,48]{1,0:T(4,128)} %price_ref.1, ...), custom_call_target="tpu_custom_call" | custom-call | tf_op jit(solution)/shard_map/pallas_call | solution.py:261
  22.6 1.4 %shard_map.113 = (f32[16,384]{1,0:T(8,128)}, f32[4,48]{1,0:T(4,128)}, f32[16,48]{1,0:T(8,128)}) custom-call(f32[16,384]{1,0:T(8,128)} %get-tuple-element.6.refs_0_, f32[4,48]{1,0:T(4,128)} %get-tuple-element.7.refs_1_, f32[16,48]{1,0:T(8,128)} %get-tuple-element.8.refs_2_), custom_call_target="tpu_custom_call" | custom-call | tf_op jit(solution)/shard_map/pallas_call | solution.py:284

commit v3 on v2

--- a/solution.py
+++ b/solution.py
@@ -35,13 +35,13 @@
     zones_all,
     factor_ref,
     plant_ref,
-    offset_ref,
-    plan_ref,
-    demand_ref,
-    price_ref,
-    mult_ref,
-    near_ref,
-    loop_ref,
+    offset_hbm,
+    plan_hbm,
+    demand_hbm,
+    price_hbm,
+    mult_hbm,
+    near_hbm,
+    loop_hbm,
     control_out,
     price_out,
     mult_out,
@@ -53,6 +53,14 @@
     heard,
     floor_message,
     floor_heard,
+    offset_ref,
+    plan_ref,
+    demand_ref,
+    price_ref,
+    mult_ref,
+    near_ref,
+    loop_ref,
+    small_sem,
     plant_sem,
     factor_sem,
     send_sem,
@@ -75,7 +83,13 @@
         factor_copies.append(
             pltpu.make_async_copy(factor_ref.at[part], factor.at[part], factor_sem.at[i])
         )
-    for copy in plant_copies + factor_copies:
+    sources = (loop_hbm, near_hbm, mult_hbm, demand_hbm, price_hbm, plan_hbm, offset_hbm)
+    targets = (loop_ref, near_ref, mult_ref, demand_ref, price_ref, plan_ref, offset_ref)
+    small = [
+        pltpu.make_async_copy(source, target, small_sem.at[i])
+        for i, (source, target) in enumerate(zip(sources, targets))
+    ]
+    for copy in small + plant_copies + factor_copies:
         copy.start()
 
     zone_peers = [(my_floor, lax.rem(me + d, cols)) for d in range(1, cols)]
@@ -120,6 +134,8 @@
         )
 
     is_load = (lane >= base) & (lane < base + groups * loops)
+    for copy in small:
+        copy.wait()
     demand = pack(demand_ref[...], base)
     price = pack(price_ref[...], base)
     mult = pack(mult_ref[...], 0)
@@ -254,14 +270,14 @@
     def local(factor, plant, offset, plan, demand, price, mult, near, loop):
         zones = plan.shape[0]
         assert (zones + loop_count(demand)) * demand.shape[1] // SUB <= LANE
-        vmem, smem = pl.BlockSpec(memory_space=pltpu.VMEM), pl.BlockSpec(memory_space=pltpu.SMEM)
-        anywhere = pl.BlockSpec(memory_space=pl.ANY)
+        vmem = pl.BlockSpec(memory_space=pltpu.VMEM)
+        hbm = pl.BlockSpec(memory_space=pltpu.HBM)
         dma = pltpu.SemaphoreType.DMA
         tile = (SUB, LANE)
         results = pl.pallas_call(
             functools.partial(kernel, floors, cols, zones * floors * cols),
-            out_shape=tuple(jax.ShapeDtypeStruct(x.shape, x.dtype) for x in (plan, price, mult)),
-            in_specs=[anywhere, anywhere, vmem, vmem, vmem, vmem, vmem, smem, smem],
+            out_shape=tuple(pltpu.VMEM(x.shape, x.dtype) for x in (plan, price, mult)),
+            in_specs=[hbm] * 9,
             out_specs=(vmem, vmem, vmem),
             scratch_shapes=[
                 pltpu.VMEM(factor.shape, jnp.float32),
@@ -272,6 +288,14 @@
                 pltpu.VMEM((ITERS, cols - 1) + tile, jnp.float32),
                 pltpu.VMEM((ITERS,) + tile, jnp.float32),
                 pltpu.VMEM((ITERS, floors - 1) + tile, jnp.float32),
+                pltpu.VMEM(offset.shape, jnp.float32),
+                pltpu.VMEM(plan.shape, jnp.float32),
+                pltpu.VMEM(demand.shape, jnp.float32),
+                pltpu.VMEM(price.shape, jnp.float32),
+                pltpu.VMEM(mult.shape, jnp.float32),
+                pltpu.SMEM(near.shape[::-1], jnp.int32),
+                pltpu.SMEM(loop.shape, jnp.int32),
+                dma((7,)),
                 dma((CHUNKS,)),
                 dma((CHUNKS,)),
                 dma((ITERS, cols - 1)),
@@ -279,13 +303,19 @@
                 dma((ITERS, floors - 1)),
                 dma((ITERS, floors - 1)),
             ],
-            compiler_params=pltpu.CompilerParams(collective_id=0, has_side_effects=True),
-        )(factor, plant, offset, plan, demand, price, mult, near.T, loop)
+            compiler_params=pltpu.CompilerParams(
+                collective_id=0, has_side_effects=True
+            ),
+        )(*(
+            pltpu.with_memory_space_constraint(x, pltpu.HBM)
+            for x in (factor, plant, offset, plan, demand, price, mult, near.T, loop)
+        ))
         return pl.pallas_call(
             hand_over,
             out_shape=tuple(jax.ShapeDtypeStruct(x.shape, x.dtype) for x in results),
             in_specs=[vmem] * 3,
             out_specs=(vmem,) * 3,
+            compiler_params=pltpu.CompilerParams(vmem_limit_bytes=2**20),
         )(*results)
 
     def loop_count(demand):

time: 24.3 us -> 22 us (0.905)
  Pallas kernels: 23.4 us -> 21.2 us
    pallas_call x1, Pallas kernels: 22 us -> 20.6 us  [local(): pl.pallas_call(functools.partial(kernel, floors, cols, zones * floors * c...]
    pallas_call x1, Pallas kernels: 1.36 us -> 0.62 us  [local(): pl.pallas_call(hand_over, out_shape=tuple((jax.ShapeDtypeStruct(x.shape,...]
where the time goes in v3:
time: 22 us; the launch traced here: 21.9 us
  Pallas kernels  21.2 us (96%)
  between operations  0.64 us (3%)
    pallas_call x1, Pallas kernels, local(): pl.pallas_call(functools.partial(kernel, floors, cols, zones * floors * c...  20.6 us
    pallas_call x1, Pallas kernels, local(): pl.pallas_call(hand_over, out_shape=tuple((jax.ShapeDtypeStruct(x.shape,...  0.62 us

profile of v3, /device:TPU:0, one launch (start us, length us, event | category | flops | bytes accessed | tf_op | source)
XLA Modules:
  0.0 21.9 jit_solution(8844189370080814050)
XLA Ops:
  0.6 20.6 %shard_map.112 = (f32[16,384]{1,0:T(8,128)S(1)}, f32[4,48]{1,0:T(4,128)S(1)}, f32[16,48]{1,0:T(8,128)S(1)}) custom-call(f32[16,96,384]{2,1,0:T(8,128)} %factor_ref.1, f32[16,96,384]{2,1,0:T(8,128)} %plant_ref.1, f32[16,384]{1,0:T(8,128)} %offset_hbm.1, f32[16,384]{1,0:T(8,128)} %plan_hbm.1, f32[4,48]{1,0:T(4,128)} %demand_hbm.1, f32[4,48]{1,0:T(4,128)} %price_hbm.1, ...), custom_call_target="tpu_custom_call" | custom-call | tf_op jit(solution)/shard_map/pallas_call | solution.py:277
  21.3 0.6 %shard_map.113 = (f32[16,384]{1,0:T(8,128)}, f32[4,48]{1,0:T(4,128)}, f32[16,48]{1,0:T(8,128)}) custom-call(f32[16,384]{1,0:T(8,128)S(1)} %get-tuple-element.6.refs_0_, f32[4,48]{1,0:T(4,128)S(1)} %get-tuple-element.7.refs_1_, f32[16,48]{1,0:T(8,128)S(1)} %get-tuple-element.8.refs_2_), custom_call_target="tpu_custom_call" | custom-call | tf_op jit(solution)/shard_map/pallas_call | solution.py:313

commit v4 on v3

--- a/solution.py
+++ b/solution.py
@@ -11,6 +11,7 @@
 MESH = pl.DeviceIdType.MESH
 SUB, LANE = 8, 128
 CHUNKS = 4
+PER_ROW = 4
 
 
 def pieces(x):
@@ -51,8 +52,8 @@
     select,
     message,
     heard,
-    floor_message,
-    floor_heard,
+    brief,
+    far_heard,
     offset_ref,
     plan_ref,
     demand_ref,
@@ -65,8 +66,8 @@
     factor_sem,
     send_sem,
     recv_sem,
-    floor_send_sem,
-    floor_recv_sem,
+    far_send_sem,
+    far_recv_sem,
 ):
     zones, rows, width = plant.shape
     horizon = rows // 2
@@ -92,10 +93,13 @@
     for copy in small + plant_copies + factor_copies:
         copy.start()
 
-    zone_peers = [(my_floor, lax.rem(me + d, cols)) for d in range(1, cols)]
-    floor_peers = [(lax.rem(my_floor + d, floors), me) for d in range(1, floors)]
+    order = sorted(range(cols), key=lambda d: -min(d, cols - d))
+    zone_peers = [(my_floor, lax.rem(me + d, cols)) for d in order[:-1]]
+    far_peers = [
+        (lax.rem(my_floor + f, floors), lax.rem(me + d, cols)) for f in range(1, floors) for d in order
+    ]
     barrier = pltpu.get_barrier_semaphore()
-    for peer in zone_peers + floor_peers:
+    for peer in zone_peers + far_peers:
         pl.semaphore_signal(barrier, inc=1, device_id=peer, device_id_type=MESH)
 
     lane = lax.broadcasted_iota(jnp.int32, (SUB, LANE), 1)
@@ -166,9 +170,38 @@
     wanted = base + (col // zones) * loops + jnp.broadcast_to(loop_lane, (LANE, LANE))
     loop_pick = ((row == wanted) & (col < base)).astype(jnp.float32).astype(jnp.bfloat16)
 
+    block = LANE // PER_ROW
+    sub = lax.broadcasted_iota(jnp.int32, (SUB, LANE), 0)
+
+    def narrow(tile):
+        rolled = tile
+        for q in range(1, PER_ROW):
+            rolled = jnp.where(lax.rem(sub, PER_ROW) == q, pltpu.roll(tile, block * q, 1), rolled)
+        return jnp.concatenate(
+            [
+                jnp.sum(rolled[PER_ROW * r : PER_ROW * (r + 1)], axis=0, keepdims=True)
+                for r in range(SUB // PER_ROW)
+            ],
+            axis=0,
+        )
+
+    def widen(pair):
+        spread = jnp.concatenate(
+            [
+                jnp.broadcast_to(pair[r : r + 1], (PER_ROW, LANE))
+                for r in range(SUB // PER_ROW)
+            ],
+            axis=0,
+        )
+        out = spread
+        for q in range(1, PER_ROW):
+            out = jnp.where(lax.rem(sub, PER_ROW) == q, pltpu.roll(spread, LANE - block * q, 1), out)
+        return out
+
     loop_of = [loop_ref[z] for z in range(zones)]
     slots = cols - 1
-    floor_slots = floors - 1
+    order_slot = {d: i for i, d in enumerate(order)}
+    far_slots = len(far_peers)
     sends = []
     for step in range(ITERS):
         source = plan_ref if step == 0 else control
@@ -192,9 +225,22 @@
                 tile = jnp.where(mine, bound, tile)
                 loads += jnp.where(lane == base + loops * j + loop_of[z], share, 0.0)
         tile = tile + loads
+        brief[step] = narrow(loads)
         message[step] = tile
         if step == 0:
-            pl.semaphore_wait(barrier, slots + floor_slots)
+            pl.semaphore_wait(barrier, slots + far_slots)
+        far_sends = []
+        for i, peer in enumerate(far_peers):
+            copy = pltpu.make_async_remote_copy(
+                src_ref=brief.at[step],
+                dst_ref=far_heard.at[step, i],
+                send_sem=far_send_sem.at[step, i],
+                recv_sem=far_recv_sem.at[step, i],
+                device_id=peer,
+                device_id_type=MESH,
+            )
+            copy.start()
+            far_sends.append(copy)
         for d in range(1, cols):
             copy = pltpu.make_async_remote_copy(
                 src_ref=message.at[step],
@@ -208,33 +254,21 @@
             sends.append(copy)
         for copy in sends[len(sends) - slots :]:
             copy.wait_recv()
-        floor_tile = tile
+        total = tile
         for d in range(slots):
-            floor_tile += heard[step, d]
-        floor_message[step] = floor_tile
-        floor_sends = []
-        for d in range(1, floors):
-            copy = pltpu.make_async_remote_copy(
-                src_ref=floor_message.at[step],
-                dst_ref=floor_heard.at[step, d - 1],
-                send_sem=floor_send_sem.at[step, d - 1],
-                recv_sem=floor_recv_sem.at[step, d - 1],
-                device_id=floor_peers[d - 1],
-                device_id_type=MESH,
-            )
-            copy.start()
-            floor_sends.append(copy)
-        everyone = jnp.concatenate([tile] + [heard[step, d] for d in range(slots)], axis=1)
+            total += heard[step, d]
+        everyone = jnp.concatenate([tile] + [heard[step, order_slot[d]] for d in range(1, cols)], axis=1)
         near = exact_dot(everyone, select[...])
         here = jnp.where(lane < base, tile, 0.0)
         target_bound = (here + near) * 0.5 - mult
         mult = mult + (here - near) * 0.5
-        for copy in floor_sends:
+        for copy in far_sends:
             copy.wait_recv()
-        sends += floor_sends
-        total = floor_tile
-        for d in range(floor_slots):
-            total += floor_heard[step, d]
+        sends += far_sends
+        far = far_heard[step, 0]
+        for i in range(1, far_slots):
+            far += far_heard[step, i]
+        total += widen(far)
         excess = jnp.where(is_load, (total - demand) * (loops / zones_all), 0.0)
         target_share = shares - exact_dot(excess + price, loop_pick)
         price = price + excess
@@ -274,6 +308,7 @@
         hbm = pl.BlockSpec(memory_space=pltpu.HBM)
         dma = pltpu.SemaphoreType.DMA
         tile = (SUB, LANE)
+        far = (floors - 1) * cols
         results = pl.pallas_call(
             functools.partial(kernel, floors, cols, zones * floors * cols),
             out_shape=tuple(pltpu.VMEM(x.shape, x.dtype) for x in (plan, price, mult)),
@@ -286,8 +321,8 @@
                 pltpu.VMEM((cols * LANE, LANE), jnp.bfloat16),
                 pltpu.VMEM((ITERS,) + tile, jnp.float32),
                 pltpu.VMEM((ITERS, cols - 1) + tile, jnp.float32),
-                pltpu.VMEM((ITERS,) + tile, jnp.float32),
-                pltpu.VMEM((ITERS, floors - 1) + tile, jnp.float32),
+                pltpu.VMEM((ITERS, SUB // PER_ROW, LANE), jnp.float32),
+                pltpu.VMEM((ITERS, far, SUB // PER_ROW, LANE), jnp.float32),
                 pltpu.VMEM(offset.shape, jnp.float32),
                 pltpu.VMEM(plan.shape, jnp.float32),
                 pltpu.VMEM(demand.shape, jnp.float32),
@@ -300,8 +335,8 @@
                 dma((CHUNKS,)),
                 dma((ITERS, cols - 1)),
                 dma((ITERS, cols - 1)),
-                dma((ITERS, floors - 1)),
-                dma((ITERS, floors - 1)),
+                dma((ITERS, far)),
+                dma((ITERS, far)),
             ],
             compiler_params=pltpu.CompilerParams(
                 collective_id=0, has_side_effects=True

time: 22 us -> 20.9 us (0.950)
  Pallas kernels: 21.2 us -> 20.1 us
    pallas_call x1, Pallas kernels: 20.6 us -> 19.4 us  [local(): pl.pallas_call(functools.partial(kernel, floors, cols, zones * floors * c...]
where the time goes in v4:
time: 20.9 us; the launch traced here: 20.7 us
  Pallas kernels  20.1 us (96%)
  between operations  0.64 us (3%)
    pallas_call x1, Pallas kernels, local(): pl.pallas_call(functools.partial(kernel, floors, cols, zones * floors * c...  19.4 us
    pallas_call x1, Pallas kernels, local(): pl.pallas_call(hand_over, out_shape=tuple((jax.ShapeDtypeStruct(x.shape,...  0.62 us

profile of v4, /device:TPU:0, one launch (start us, length us, event | category | flops | bytes accessed | tf_op | source)
XLA Modules:
  0.0 20.7 jit_solution(1194554480175240434)
XLA Ops:
  0.6 19.4 %shard_map.112 = (f32[16,384]{1,0:T(8,128)S(1)}, f32[4,48]{1,0:T(4,128)S(1)}, f32[16,48]{1,0:T(8,128)S(1)}) custom-call(f32[16,96,384]{2,1,0:T(8,128)} %factor_ref.1, f32[16,96,384]{2,1,0:T(8,128)} %plant_ref.1, f32[16,384]{1,0:T(8,128)} %offset_hbm.1, f32[16,384]{1,0:T(8,128)} %plan_hbm.1, f32[4,48]{1,0:T(4,128)} %demand_hbm.1, f32[4,48]{1,0:T(4,128)} %price_hbm.1, ...), custom_call_target="tpu_custom_call" | custom-call | tf_op jit(solution)/shard_map/pallas_call | solution.py:312
  20.1 0.6 %shard_map.113 = (f32[16,384]{1,0:T(8,128)}, f32[4,48]{1,0:T(4,128)}, f32[16,48]{1,0:T(8,128)}) custom-call(f32[16,384]{1,0:T(8,128)S(1)} %get-tuple-element.6.refs_0_, f32[4,48]{1,0:T(4,128)S(1)} %get-tuple-element.7.refs_1_, f32[16,48]{1,0:T(8,128)S(1)} %get-tuple-element.8.refs_2_), custom_call_target="tpu_custom_call" | custom-call | tf_op jit(solution)/shard_map/pallas_call | solution.py:348

commit v5 on v4

--- a/solution.py
+++ b/solution.py
@@ -50,6 +50,7 @@
     plant,
     control,
     select,
+    bound_part,
     message,
     heard,
     brief,
@@ -90,7 +91,7 @@
         pltpu.make_async_copy(source, target, small_sem.at[i])
         for i, (source, target) in enumerate(zip(sources, targets))
     ]
-    for copy in small + plant_copies + factor_copies:
+    for copy in small + plant_copies:
         copy.start()
 
     order = sorted(range(cols), key=lambda d: -min(d, cols - d))
@@ -99,8 +100,10 @@
         (lax.rem(my_floor + f, floors), lax.rem(me + d, cols)) for f in range(1, floors) for d in order
     ]
     barrier = pltpu.get_barrier_semaphore()
-    for peer in zone_peers + far_peers:
+    for peer in far_peers + zone_peers:
         pl.semaphore_signal(barrier, inc=1, device_id=peer, device_id_type=MESH)
+    for copy in factor_copies:
+        copy.start()
 
     lane = lax.broadcasted_iota(jnp.int32, (SUB, LANE), 1)
 
@@ -196,6 +199,15 @@
         out = spread
         for q in range(1, PER_ROW):
             out = jnp.where(lax.rem(sub, PER_ROW) == q, pltpu.roll(spread, LANE - block * q, 1), out)
+        return out
+
+    def half_sum(target, z, half):
+        out = jnp.zeros((SUB, width), jnp.float32)
+        for j in range(groups):
+            at = zones * j + z
+            column = jnp.broadcast_to(target[:, at : at + 1], (SUB, width))
+            first = half * horizon + SUB * j
+            out += factor[z, first : first + SUB, :] * column
         return out
 
     loop_of = [loop_ref[z] for z in range(zones)]
@@ -262,6 +274,10 @@
         here = jnp.where(lane < base, tile, 0.0)
         target_bound = (here + near) * 0.5 - mult
         mult = mult + (here - near) * 0.5
+        for z in range(zones):
+            if step == 0 and z % step_zones == 0:
+                factor_copies[z // step_zones].wait()
+            bound_part[z] = half_sum(target_bound, z, 1)
         for copy in far_sends:
             copy.wait_recv()
         sends += far_sends
@@ -273,16 +289,8 @@
         target_share = shares - exact_dot(excess + price, loop_pick)
         price = price + excess
         for z in range(zones):
-            if step == 0 and z % step_zones == 0:
-                factor_copies[z // step_zones].wait()
-            total_z = jnp.zeros((SUB, width), jnp.float32)
-            for half, target in enumerate((target_share, target_bound)):
-                for j in range(groups):
-                    at = zones * j + z
-                    column = jnp.broadcast_to(target[:, at : at + 1], (SUB, width))
-                    first = half * horizon + SUB * j
-                    total_z += factor[z, first : first + SUB, :] * column
-            result = 0.8 * jnp.sum(total_z, axis=0, keepdims=True) - offset_ref[z : z + 1, :]
+            result_sum = bound_part[z] + half_sum(target_share, z, 0)
+            result = 0.8 * jnp.sum(result_sum, axis=0, keepdims=True) - offset_ref[z : z + 1, :]
             if step == ITERS - 1:
                 control_out[z : z + 1, :] = result
             else:
@@ -319,6 +327,7 @@
                 pltpu.VMEM(plant.shape, jnp.float32),
                 pltpu.VMEM(plan.shape, jnp.float32),
                 pltpu.VMEM((cols * LANE, LANE), jnp.bfloat16),
+                pltpu.VMEM((zones, SUB, factor.shape[2]), jnp.float32),
                 pltpu.VMEM((ITERS,) + tile, jnp.float32),
                 pltpu.VMEM((ITERS, cols - 1) + tile, jnp.float32),
                 pltpu.VMEM((ITERS, SUB // PER_ROW, LANE), jnp.float32),

time: 20.9 us -> 20.1 us (0.962)
  Pallas kernels: 20.1 us -> 19.3 us
    pallas_call x1, Pallas kernels: 19.4 us -> 18.7 us  [local(): pl.pallas_call(functools.partial(kernel, floors, cols, zones * floors * c...]
where the time goes in v5:
time: 20.1 us; the launch traced here: 20 us
  Pallas kernels  19.3 us (96%)
  between operations  0.64 us (3%)
    pallas_call x1, Pallas kernels, local(): pl.pallas_call(functools.partial(kernel, floors, cols, zones * floors * c...  18.7 us
    pallas_call x1, Pallas kernels, local(): pl.pallas_call(hand_over, out_shape=tuple((jax.ShapeDtypeStruct(x.shape,...  0.62 us

profile of v5, /device:TPU:0, one launch (start us, length us, event | category | flops | bytes accessed | tf_op | source)
XLA Modules:
  0.0 20.0 jit_solution(6748240214133080420)
XLA Ops:
  0.6 18.7 %shard_map.112 = (f32[16,384]{1,0:T(8,128)S(1)}, f32[4,48]{1,0:T(4,128)S(1)}, f32[16,48]{1,0:T(8,128)S(1)}) custom-call(f32[16,96,384]{2,1,0:T(8,128)} %factor_ref.1, f32[16,96,384]{2,1,0:T(8,128)} %plant_ref.1, f32[16,384]{1,0:T(8,128)} %offset_hbm.1, f32[16,384]{1,0:T(8,128)} %plan_hbm.1, f32[4,48]{1,0:T(4,128)} %demand_hbm.1, f32[4,48]{1,0:T(4,128)} %price_hbm.1, ...), custom_call_target="tpu_custom_call" | custom-call | tf_op jit(solution)/shard_map/pallas_call | solution.py:320
  19.4 0.6 %shard_map.113 = (f32[16,384]{1,0:T(8,128)}, f32[4,48]{1,0:T(4,128)}, f32[16,48]{1,0:T(8,128)}) custom-call(f32[16,384]{1,0:T(8,128)S(1)} %get-tuple-element.6.refs_0_, f32[4,48]{1,0:T(4,128)S(1)} %get-tuple-element.7.refs_1_, f32[16,48]{1,0:T(8,128)S(1)} %get-tuple-element.8.refs_2_), custom_call_target="tpu_custom_call" | custom-call | tf_op jit(solution)/shard_map/pallas_call | solution.py:357
